TPU v7x, 32 devices: a whole 2x2x4 slice. The times are simulated.
32 devices in a mesh: gx: 8 (over y, x, core), gy: 4 (over z).
Axes of the slice: x: 2, y: 2, z: 4, core: 2. Of those that a mesh axis runs over, the one named last changes fastest.
Arguments:
- probes: bfloat16 [256, 1024, 256], P('gx', 'gy'), may hold values from -6 to 6
- blk_rows: int32 [1024, 128], P(('gx', 'gy')), may hold values from 0 to 8191
- blk_sensor: int32 [1024], P(('gx', 'gy')), may hold values from 0 to 255, as said below
- blk_count: int32 [32], P(('gx', 'gy')), may hold values from 16 to 32, as said below
- coef: bfloat16 [1024, 128], P(('gx', 'gy')), may hold values from -5 to 5
- owner: int32 [256], replicated, may hold values from 0 to 31, as said below
- weights: float32 [256], replicated, may hold values from 0.1 to 1
Outputs:
- sensitivity: float32 [256], P(('gx', 'gy'))
- new_weights: float32 [256], replicated
- density: float32 [256, 1024], P('gx', 'gy')
Inputs may be any that keep to these rules, and one draw needn't show every extreme that they name: `owner`: every device owns exactly 8 sensors. `blk_sensor`: among the live slots of one tile, at most 2 belong to sensors of one owner; in every draw some owner receives 2 live blocks from every tile. `blk_count`: some tile has all 32 slots live.
All inputs are finite; a program needn't handle non-finite values.
Results may differ from a plain program's by a relative error of at most 0.0008.
Values may be sent and summed in bfloat16 or wider, within the bound.
A program may use at most 128 MiB of HBM per device.

v0:
```python
import jax
import jax.numpy as jnp
from jax import lax
from jax.sharding import PartitionSpec as P

SPD = 8
CAP = 2


def local(probes, blk_rows, blk_sensor, blk_count, coef, owner, weights):
    size_gx = lax.axis_size("gx")
    size_gy = lax.axis_size("gy")
    n_dev = size_gx * size_gy
    me_flat = lax.axis_index("gx") * size_gy + lax.axis_index("gy")
    tile_r, tile_c, probe_n = probes.shape
    nblk, foot = blk_rows.shape
    n_sens = owner.shape[0]
    flat = probes.reshape(tile_r * tile_c, probe_n)
    picked = flat[blk_rows.reshape(-1)].reshape(nblk, foot, probe_n)
    slots = jnp.arange(nblk, dtype=jnp.int32)
    alive = slots < blk_count[0]
    dest = owner[blk_sensor]
    earlier = (dest[:, None] == dest[None, :]) & alive[None, :] & (slots[None, :] < slots[:, None])
    rank = jnp.sum(earlier.astype(jnp.int32), axis=1)
    position = jnp.where(alive, dest * CAP + rank, n_dev * CAP)
    send_rows = (
        jnp.zeros((n_dev * CAP, foot, probe_n), jnp.bfloat16).at[position].set(picked, mode="drop")
    )
    send_coef = jnp.zeros((n_dev * CAP, foot), jnp.bfloat16).at[position].set(coef, mode="drop")
    send_ids = jnp.full((n_dev * CAP,), -1, jnp.int32).at[position].set(blk_sensor, mode="drop")
    recv_rows, recv_coef, recv_ids = (
        lax.all_to_all(send_rows, ("gx", "gy"), split_axis=0, concat_axis=0, tiled=True),
        lax.all_to_all(send_coef, ("gx", "gy"), split_axis=0, concat_axis=0, tiled=True),
        lax.all_to_all(send_ids, ("gx", "gy"), split_axis=0, concat_axis=0, tiled=True),
    )
    my_ids = jnp.nonzero(owner == me_flat, size=SPD, fill_value=0)[0].astype(jnp.int32)
    select = (recv_ids[None, :] == my_ids[:, None]).astype(jnp.bfloat16)
    mixer = select[:, :, None] * recv_coef[None, :, :]
    obs = jnp.einsum("ksr,srp->krp", mixer, recv_rows, preferred_element_type=jnp.float32)
    owned = jnp.sum(obs * obs, axis=(1, 2)) / (foot * probe_n)
    spread = jnp.zeros((n_sens,), jnp.float32).at[my_ids].set(owned)
    sens_all = lax.psum(spread, ("gx", "gy"))
    gain = weights * jnp.sqrt(1.0 + sens_all)
    new_weights = n_sens * gain / jnp.sum(gain)
    values_pts = jnp.where(
        alive[:, None], new_weights[blk_sensor][:, None] * jnp.square(coef.astype(jnp.float32)), 0.0
    )
    density = (
        jnp.zeros((tile_r * tile_c,), jnp.float32)
        .at[blk_rows.reshape(-1)]
        .add(values_pts.reshape(-1))
    )
    return (owned, new_weights, density.reshape(tile_r, tile_c))


def solution(mesh):
    in_specs = (
        P("gx", "gy", None),
        P(("gx", "gy"), None),
        P(("gx", "gy")),
        P(("gx", "gy")),
        P(("gx", "gy"), None),
        P(),
        P(),
    )
    out_specs = (P(("gx", "gy")), P(), P("gx", "gy"))
    return jax.shard_map(local, mesh=mesh, in_specs=in_specs, out_specs=out_specs, check_vma=False)
```

profile of v0, /device:TPU:0, one launch (start us, length us, event | category | flops | bytes accessed | tf_op | source)
XLA Modules:
  0.0 216.1 jit_solution(14006273843416477223)
XLA Ops:
  0.6 0.7 compare_select_fusion.4
  2.0 1.4 gather_fusion
  3.4 0.2 convert_reduce_fusion
  3.5 0.8 scatter_custom_fusion.1
  4.4 0.7 all_to_all.16
  5.1 7.3 %all-to-all-start.1 = ((s32[32,2,1]{1,2,0:T(1,128)}), s32[32,2,1]{1,2,0:T(1,128)S(1)}, u32[]{:S(2)}, u32[]{:S(2)}) async-start(s32[32,2,1]{1,2,0:T(1,128)} %bitcast.7), calls=%async_computation.1 | async-start | bytes 32768 | tf_op jit(solution)/shard_map/all_to_all | solution.py:34
  12.4 0.7 compare_select_fusion
  13.1 1.4 scatter_custom_fusion.3
  14.5 5.1 %all-to-all-done.1 = s32[32,2,1]{1,2,0:T(1,128)S(1)} async-done(((s32[32,2,1]{1,2,0:T(1,128)}), s32[32,2,1]{1,2,0:T(1,128)S(1)}, u32[]{:S(2)}, u32[]{:S(2)}) %all-to-all-start.1) | async-done | bytes 288 | tf_op jit(solution)/shard_map/all_to_all | solution.py:34
  19.6 2.5 %all-to-all-start.2 = ((bf16[32,2,128]{2,1,0:T(2,128)(2,1)}), bf16[32,2,128]{2,1,0:T(2,128)(2,1)S(1)}, u32[]{:S(2)}, u32[]{:S(2)}) async-start(bf16[32,2,128]{2,1,0:T(2,128)(2,1)} %bitcast.13), calls=%async_computation.2 | async-start | bytes 32768 | tf_op jit(solution)/shard_map/all_to_all | solution.py:33
  22.2 15.7 %gather_fusion.1 = bf16[4096,256]{1,0:T(8,128)(2,1)S(1)} fusion(bf16[8192,256]{1,0:T(8,128)(2,1)} %bitcast.28, s32[4096]{0:T(1024)S(1)} %broadcast_clamp_fusion), kind=kCustom, calls=%fused_computation.1 | custom fusion | bytes 4210688 | tf_op jit(solution)/shard_map/gather | solution.py:19
  37.9 2.5 %broadcast_in_dim.36 = bf16[64,128,256]{2,1,0:T(8,128)(2,1)} broadcast(bf16[]{:T(256)} %constant.26.clone.1), dimensions={} | broadcast | bytes 4194306 | tf_op jit(solution)/shard_map/broadcast_in_dim | solution.py:27
  40.4 5.3 %scatter_fusion = bf16[64,128,256]{2,1,0:T(8,128)(2,1)} fusion(bf16[64,128,256]{2,1,0:T(8,128)(2,1)} %broadcast_in_dim.36, s32[32]{0:T(128)S(1)} %fusion.23, bf16[32,128,256]{2,1,0:T(8,128)(2,1)S(1)} %bitcast.29), kind=kCustom, calls=%fused_computation.3 | custom fusion | bytes 6291584 | tf_op jit(solution)/shard_map/scatter | solution.py:27
  45.7 0.0 copy-start
  45.7 0.0 all-to-all-done.2
  45.7 6.3 %all-to-all-start = ((bf16[64,128,256]{2,1,0:T(8,128)(2,1)}), bf16[64,128,256]{2,1,0:T(8,128)(2,1)}, u32[]{:S(2)}, u32[]{:S(2)}) async-start(bf16[64,128,256]{2,1,0:T(8,128)(2,1)} %scatter_fusion), calls=%async_computation | async-start | bytes 8388608 | tf_op jit(solution)/shard_map/all_to_all | solution.py:32
  52.0 0.0 copy-start.3
  52.0 0.0 copy-start.2
  52.0 0.0 copy-done
  52.1 0.3 reduce-window.12
  52.4 0.1 slice.7
  52.5 0.1 slice_reduce_fusion
  52.6 0.1 broadcast_add_fusion
  52.7 2.3 %scatter_custom_fusion.2 = s32[8]{0:T(128)S(1)} fusion(s32[256]{0:T(256)S(1)} %bitcast.35, s32[256]{0:T(256)S(1)} %broadcast.233, s32[]{:T(128)} %constant.27.clone.1), kind=kCustom, calls=%fused_computation.56 | custom fusion | flops 256 | bytes 36 | tf_op jit(solution)/shard_map/scatter-add | solution.py:36
  55.0 0.2 select_n.113
  55.2 0.6 fusion.17
  55.8 0.7 compare_select_fusion.10
  56.5 0.7 fusion.20
  57.2 0.5 broadcast.255
  57.7 0.7 reduce.6
  58.4 0.1 eq.43
  58.5 0.1 compare_convert_fusion
  58.5 0.1 copy.16
  58.7 85.6 %all-to-all-done = bf16[64,128,256]{2,1,0:T(8,128)(2,1)} async-done(((bf16[64,128,256]{2,1,0:T(8,128)(2,1)}), bf16[64,128,256]{2,1,0:T(8,128)(2,1)}, u32[]{:S(2)}, u32[]{:S(2)}) %all-to-all-start) | async-done | bytes 4194336 | tf_op jit(solution)/shard_map/all_to_all | solution.py:32
  144.2 4.6 %fusion.5 = f32[8]{0:T(128)S(1)} fusion(bf16[64,128,256]{2,1,0:T(8,128)(2,1)} %all-to-all-done, bf16[64,128]{0,1:T(8,128)(2,1)S(1)} %copy.16, bf16[8,64]{1,0:T(8,128)(2,1)S(1)} %compare_convert_fusion), kind=kOutput, calls=%fused_computation.12 | convolution fusion | flops 34144248 | bytes 4211744 | tf_op jit(solution)/shard_map/ksr,srp->krp/dot_general | solution.py:39
  148.8 0.0 copy-start.4
  148.9 0.6 scatter_custom_fusion.4
  149.5 42.0 %psum.7 = f32[256]{0:T(256)S(1)} all-reduce(f32[256]{0:T(256)S(1)} %scatter_custom_fusion.4), channel_id=1, replica_groups=mesh['gx'=8,'gy'=4] {'gx','gy'}, use_global_device_ids=true, to_apply=%region_11.12 | all-reduce | flops 256 | bytes 2048 | tf_op jit(solution)/shard_map/psum | solution.py:42
  191.5 0.0 copy-done.3
  191.5 0.6 fusion.28
  192.1 0.7 multiply_divide_fusion
  192.7 0.0 copy-start.1
  192.7 0.7 gather_fusion.2
  193.4 0.0 copy-done.2
  193.4 0.1 select_bitcast_fusion
  193.5 21.9 %scatter_custom_fusion.5 = f32[8192]{0:T(1024)S(1)} fusion(s32[4096]{0:T(1024)S(1)} %bitcast.32, f32[4096]{0:T(1024)S(1)} %select_bitcast_fusion, f32[]{:T(128)} %constant.76.clone.1), kind=kCustom, calls=%fused_computation.18 | custom fusion | flops 4096 | bytes 32772 | tf_op jit(solution)/shard_map/scatter-add | solution.py:51
  215.5 0.6 reshape.248
  216.1 0.0 copy-done.4
  216.1 0.0 copy-done.1
  (9 shorter events, 0.1 us)
Async XLA Ops:
  5.1 14.5 %all-to-all-start.1 = ((s32[32,2,1]{1,2,0:T(1,128)}), s32[32,2,1]{1,2,0:T(1,128)S(1)}, u32[]{:S(2)}, u32[]{:S(2)}) async-start(s32[32,2,1]{1,2,0:T(1,128)} %bitcast.7), calls=%async_computation.1 | async-start | bytes 32768 | tf_op jit(solution)/shard_map/all_to_all | solution.py:34
  19.6 26.1 %all-to-all-start.2 = ((bf16[32,2,128]{2,1,0:T(2,128)(2,1)}), bf16[32,2,128]{2,1,0:T(2,128)(2,1)S(1)}, u32[]{:S(2)}, u32[]{:S(2)}) async-start(bf16[32,2,128]{2,1,0:T(2,128)(2,1)} %bitcast.13), calls=%async_computation.2 | async-start | bytes 32768 | tf_op jit(solution)/shard_map/all_to_all | solution.py:33
  45.7 6.4 %copy-start = (s32[256]{0:T(256)S(1)}, s32[256]{0:T(256)}, u32[]{:S(2)}) copy-start(s32[256]{0:T(256)} %param.12) | copy-start | bytes 3076
  45.7 98.6 %all-to-all-start = ((bf16[64,128,256]{2,1,0:T(8,128)(2,1)}), bf16[64,128,256]{2,1,0:T(8,128)(2,1)}, u32[]{:S(2)}, u32[]{:S(2)}) async-start(bf16[64,128,256]{2,1,0:T(8,128)(2,1)} %scatter_fusion), calls=%async_computation | async-start | bytes 8388608 | tf_op jit(solution)/shard_map/all_to_all | solution.py:32
  52.0 139.4 %copy-start.3 = (f32[256]{0:T(256)S(1)}, f32[256]{0:T(256)}, u32[]{:S(2)}) copy-start(f32[256]{0:T(256)} %param.13) | copy-start | bytes 3076
  52.0 141.4 %copy-start.2 = (bf16[32,128]{1,0:T(8,128)(2,1)S(1)}, bf16[32,128]{1,0:T(8,128)(2,1)}, u32[]{:S(2)}) copy-start(bf16[32,128]{1,0:T(8,128)(2,1)} %param.11) | copy-start | bytes 24580
  148.8 67.2 %copy-start.4 = (f32[8]{0:T(128)}, f32[8]{0:T(128)S(1)}, u32[]{:S(2)}) copy-start(f32[8]{0:T(128)S(1)} %broadcast_multiply_fusion) | copy-start | bytes 100
  192.7 23.4 %copy-start.1 = (f32[256]{0:T(256)}, f32[256]{0:T(256)S(1)}, u32[]{:S(2)}) copy-start(f32[256]{0:T(256)S(1)} %multiply_divide_fusion) | copy-start | bytes 3076
where the time goes:
time: 217 us; the launch traced here: 216 us
  waiting for transfers between devices  90.6 us (42%)
  blocking collectives  42 us (19%)
  local copies, waits for them, and re-layouts  30.7 us (14%)
  other arithmetic  30.5 us (14%)
  starting transfers between devices  16.2 us (7%)
  matrix products  4.62 us (2%)
    all_to_all x1, waiting for transfers between devices, local(): lax.all_to_all(send_rows, ('gx', 'gy'), split_axis=0, concat_axis=0, tile...  85.6 us
    psum x1, blocking collectives, local(): sens_all = lax.psum(spread, ('gx', 'gy'))  42 us
    scatter-add x1, other arithmetic, local(): density = jnp.zeros((tile_r * tile_c,), jnp.float32).at[blk_rows.reshape(...  21.9 us
    gather x1, local copies, waits for them, and re-layouts, local(): picked = flat[blk_rows.reshape(-1)].reshape(nblk, foot, probe_n)  15.7 us
    all_to_all x1, starting transfers between devices, local(): lax.all_to_all(send_ids, ('gx', 'gy'), split_axis=0, concat_axis=0, tiled...  7.33 us
    all_to_all x1, starting transfers between devices, local(): lax.all_to_all(send_rows, ('gx', 'gy'), split_axis=0, concat_axis=0, tile...  6.35 us
    scatter x1, local copies, waits for them, and re-layouts, local(): jnp.zeros((n_dev * CAP, foot, probe_n), jnp.bfloat16).at[position]  5.29 us
    all_to_all x1, waiting for transfers between devices, local(): lax.all_to_all(send_ids, ('gx', 'gy'), split_axis=0, concat_axis=0, tiled...  5.05 us
  transfers between devices with their start and end apart: 3, of which 2 were waited for; matrix products, arithmetic and copies ran while one was open for 15% of the time, Pallas kernels for 0%

commit v1 on v0

--- a/solution.py
+++ b/solution.py
@@ -39,7 +39,7 @@
     obs = jnp.einsum("ksr,srp->krp", mixer, recv_rows, preferred_element_type=jnp.float32)
     owned = jnp.sum(obs * obs, axis=(1, 2)) / (foot * probe_n)
     spread = jnp.zeros((n_sens,), jnp.float32).at[my_ids].set(owned)
-    sens_all = lax.psum(spread, ("gx", "gy"))
+    sens_all = lax.psum(lax.psum(spread, "gy"), "gx")
     gain = weights * jnp.sqrt(1.0 + sens_all)
     new_weights = n_sens * gain / jnp.sum(gain)
     values_pts = jnp.where(

time: 217 us -> 198 us (0.912)
  blocking collectives: 42 us -> 23.5 us
    psum x1 -> x2, blocking collectives: 42 us -> 23.5 us  [local(): sens_all = lax.psum(lax.psum(spread, 'gy'), 'gx')]
  transfers between devices with their start and end apart: 3 -> 3, of which waited for: 2 -> 2; matrix products, arithmetic and copies ran while one was open for 15% -> 16% of each run, Pallas kernels for 0% -> 0%
where the time goes in v1:
time: 198 us
  waiting for transfers between devices  90.6 us (46%)
  local copies, waits for them, and re-layouts  30.7 us (16%)
  other arithmetic  30.5 us (15%)
  blocking collectives  23.5 us (12%)
  starting transfers between devices  16.2 us (8%)
  matrix products  4.62 us (2%)
    all_to_all x1, waiting for transfers between devices, local(): lax.all_to_all(send_rows, ('gx', 'gy'), split_axis=0, concat_axis=0, tile...  85.6 us
    psum x2, blocking collectives, local(): sens_all = lax.psum(lax.psum(spread, 'gy'), 'gx')  23.5 us
    scatter-add x1, other arithmetic, local(): density = jnp.zeros((tile_r * tile_c,), jnp.float32).at[blk_rows.reshape(...  21.9 us
    gather x1, local copies, waits for them, and re-layouts, local(): picked = flat[blk_rows.reshape(-1)].reshape(nblk, foot, probe_n)  15.7 us
    all_to_all x1, starting transfers between devices, local(): lax.all_to_all(send_ids, ('gx', 'gy'), split_axis=0, concat_axis=0, tiled...  7.33 us
    all_to_all x1, starting transfers between devices, local(): lax.all_to_all(send_rows, ('gx', 'gy'), split_axis=0, concat_axis=0, tile...  6.35 us
    scatter x1, local copies, waits for them, and re-layouts, local(): jnp.zeros((n_dev * CAP, foot, probe_n), jnp.bfloat16).at[position]  5.29 us
    all_to_all x1, waiting for transfers between devices, local(): lax.all_to_all(send_ids, ('gx', 'gy'), split_axis=0, concat_axis=0, tiled...  5.05 us
  transfers between devices with their start and end apart: 3, of which 2 were waited for; matrix products, arithmetic and copies ran while one was open for 16% of the time, Pallas kernels for 0%

profile of v1, /device:TPU:0, one launch (start us, length us, event | category | flops | bytes accessed | tf_op | source)
XLA Modules:
  0.0 197.6 jit_solution(17053275645132159106)
XLA Ops:
  0.6 0.7 compare_select_fusion.4
  2.0 1.4 gather_fusion
  3.4 0.2 convert_reduce_fusion
  3.5 0.8 scatter_custom_fusion.1
  4.4 0.7 all_to_all.16
  5.1 7.3 %all-to-all-start.1 = ((s32[32,2,1]{1,2,0:T(1,128)}), s32[32,2,1]{1,2,0:T(1,128)S(1)}, u32[]{:S(2)}, u32[]{:S(2)}) async-start(s32[32,2,1]{1,2,0:T(1,128)} %bitcast.7), calls=%async_computation.1 | async-start | bytes 32768 | tf_op jit(solution)/shard_map/all_to_all | solution.py:34
  12.4 0.7 compare_select_fusion
  13.1 1.4 scatter_custom_fusion.3
  14.5 5.1 %all-to-all-done.1 = s32[32,2,1]{1,2,0:T(1,128)S(1)} async-done(((s32[32,2,1]{1,2,0:T(1,128)}), s32[32,2,1]{1,2,0:T(1,128)S(1)}, u32[]{:S(2)}, u32[]{:S(2)}) %all-to-all-start.1) | async-done | bytes 288 | tf_op jit(solution)/shard_map/all_to_all | solution.py:34
  19.6 2.5 %all-to-all-start.2 = ((bf16[32,2,128]{2,1,0:T(2,128)(2,1)}), bf16[32,2,128]{2,1,0:T(2,128)(2,1)S(1)}, u32[]{:S(2)}, u32[]{:S(2)}) async-start(bf16[32,2,128]{2,1,0:T(2,128)(2,1)} %bitcast.13), calls=%async_computation.2 | async-start | bytes 32768 | tf_op jit(solution)/shard_map/all_to_all | solution.py:33
  22.2 15.7 %gather_fusion.1 = bf16[4096,256]{1,0:T(8,128)(2,1)S(1)} fusion(bf16[8192,256]{1,0:T(8,128)(2,1)} %bitcast.28, s32[4096]{0:T(1024)S(1)} %broadcast_clamp_fusion), kind=kCustom, calls=%fused_computation.1 | custom fusion | bytes 4210688 | tf_op jit(solution)/shard_map/gather | solution.py:19
  37.9 2.5 %broadcast_in_dim.36 = bf16[64,128,256]{2,1,0:T(8,128)(2,1)} broadcast(bf16[]{:T(256)} %constant.26.clone.1), dimensions={} | broadcast | bytes 4194306 | tf_op jit(solution)/shard_map/broadcast_in_dim | solution.py:27
  40.4 5.3 %scatter_fusion = bf16[64,128,256]{2,1,0:T(8,128)(2,1)} fusion(bf16[64,128,256]{2,1,0:T(8,128)(2,1)} %broadcast_in_dim.36, s32[32]{0:T(128)S(1)} %fusion.23, bf16[32,128,256]{2,1,0:T(8,128)(2,1)S(1)} %bitcast.29), kind=kCustom, calls=%fused_computation.3 | custom fusion | bytes 6291584 | tf_op jit(solution)/shard_map/scatter | solution.py:27
  45.7 0.0 copy-start
  45.7 0.0 all-to-all-done.2
  45.7 6.3 %all-to-all-start = ((bf16[64,128,256]{2,1,0:T(8,128)(2,1)}), bf16[64,128,256]{2,1,0:T(8,128)(2,1)}, u32[]{:S(2)}, u32[]{:S(2)}) async-start(bf16[64,128,256]{2,1,0:T(8,128)(2,1)} %scatter_fusion), calls=%async_computation | async-start | bytes 8388608 | tf_op jit(solution)/shard_map/all_to_all | solution.py:32
  52.0 0.0 copy-start.3
  52.0 0.0 copy-start.2
  52.0 0.0 copy-done
  52.1 0.3 reduce-window.12
  52.4 0.1 slice.7
  52.5 0.1 slice_reduce_fusion
  52.6 0.1 broadcast_add_fusion
  52.7 2.3 %scatter_custom_fusion.2 = s32[8]{0:T(128)S(1)} fusion(s32[256]{0:T(256)S(1)} %bitcast.35, s32[256]{0:T(256)S(1)} %broadcast.233, s32[]{:T(128)} %constant.27.clone.1), kind=kCustom, calls=%fused_computation.56 | custom fusion | flops 256 | bytes 36 | tf_op jit(solution)/shard_map/scatter-add | solution.py:36
  55.0 0.2 select_n.113
  55.2 0.6 fusion.17
  55.8 0.7 compare_select_fusion.10
  56.5 0.7 fusion.20
  57.2 0.5 broadcast.255
  57.7 0.7 reduce.6
  58.4 0.1 eq.43
  58.5 0.1 compare_convert_fusion
  58.5 0.1 copy.16
  58.7 85.6 %all-to-all-done = bf16[64,128,256]{2,1,0:T(8,128)(2,1)} async-done(((bf16[64,128,256]{2,1,0:T(8,128)(2,1)}), bf16[64,128,256]{2,1,0:T(8,128)(2,1)}, u32[]{:S(2)}, u32[]{:S(2)}) %all-to-all-start) | async-done | bytes 4194336 | tf_op jit(solution)/shard_map/all_to_all | solution.py:32
  144.2 4.6 %fusion.5 = f32[8]{0:T(128)S(1)} fusion(bf16[64,128,256]{2,1,0:T(8,128)(2,1)} %all-to-all-done, bf16[64,128]{0,1:T(8,128)(2,1)S(1)} %copy.16, bf16[8,64]{1,0:T(8,128)(2,1)S(1)} %compare_convert_fusion), kind=kOutput, calls=%fused_computation.12 | convolution fusion | flops 34144248 | bytes 4211744 | tf_op jit(solution)/shard_map/ksr,srp->krp/dot_general | solution.py:39
  148.8 0.0 copy-start.4
  148.9 0.6 scatter_custom_fusion.4
  149.5 11.7 %psum.14 = f32[256]{0:T(256)S(1)} all-reduce(f32[256]{0:T(256)S(1)} %scatter_custom_fusion.4), channel_id=1, replica_groups=mesh['gx'=8,'gy'=4] {'gy'}, use_global_device_ids=true, to_apply=%region_11.12 | all-reduce | flops 256 | bytes 2048 | tf_op jit(solution)/shard_map/psum | solution.py:42
  161.2 11.8 %psum.15 = f32[256]{0:T(256)S(1)} all-reduce(f32[256]{0:T(256)S(1)} %psum.14), channel_id=1, replica_groups=mesh['gx'=8,'gy'=4] {'gx'}, use_global_device_ids=true, to_apply=%region_12.13 | all-reduce | flops 256 | bytes 2048 | tf_op jit(solution)/shard_map/psum | solution.py:42
  173.0 0.0 copy-done.3
  173.0 0.6 fusion.28
  173.6 0.7 multiply_divide_fusion
  174.2 0.0 copy-start.1
  174.3 0.7 gather_fusion.2
  175.0 0.0 copy-done.2
  175.0 0.1 select_bitcast_fusion
  175.0 21.9 %scatter_custom_fusion.5 = f32[8192]{0:T(1024)S(1)} fusion(s32[4096]{0:T(1024)S(1)} %bitcast.32, f32[4096]{0:T(1024)S(1)} %select_bitcast_fusion, f32[]{:T(128)} %constant.76.clone.1), kind=kCustom, calls=%fused_computation.18 | custom fusion | flops 4096 | bytes 32772 | tf_op jit(solution)/shard_map/scatter-add | solution.py:51
  197.0 0.6 reshape.248
  197.6 0.0 copy-done.4
  197.6 0.0 copy-done.1
  (9 shorter events, 0.1 us)
Async XLA Ops:
  5.1 14.5 %all-to-all-start.1 = ((s32[32,2,1]{1,2,0:T(1,128)}), s32[32,2,1]{1,2,0:T(1,128)S(1)}, u32[]{:S(2)}, u32[]{:S(2)}) async-start(s32[32,2,1]{1,2,0:T(1,128)} %bitcast.7), calls=%async_computation.1 | async-start | bytes 32768 | tf_op jit(solution)/shard_map/all_to_all | solution.py:34
  19.6 26.1 %all-to-all-start.2 = ((bf16[32,2,128]{2,1,0:T(2,128)(2,1)}), bf16[32,2,128]{2,1,0:T(2,128)(2,1)S(1)}, u32[]{:S(2)}, u32[]{:S(2)}) async-start(bf16[32,2,128]{2,1,0:T(2,128)(2,1)} %bitcast.13), calls=%async_computation.2 | async-start | bytes 32768 | tf_op jit(solution)/shard_map/all_to_all | solution.py:33
  45.7 6.4 %copy-start = (s32[256]{0:T(256)S(1)}, s32[256]{0:T(256)}, u32[]{:S(2)}) copy-start(s32[256]{0:T(256)} %param.12) | copy-start | bytes 3076
  45.7 98.6 %all-to-all-start = ((bf16[64,128,256]{2,1,0:T(8,128)(2,1)}), bf16[64,128,256]{2,1,0:T(8,128)(2,1)}, u32[]{:S(2)}, u32[]{:S(2)}) async-start(bf16[64,128,256]{2,1,0:T(8,128)(2,1)} %scatter_fusion), calls=%async_computation | async-start | bytes 8388608 | tf_op jit(solution)/shard_map/all_to_all | solution.py:32
  52.0 121.0 %copy-start.3 = (f32[256]{0:T(256)S(1)}, f32[256]{0:T(256)}, u32[]{:S(2)}) copy-start(f32[256]{0:T(256)} %param.13) | copy-start | bytes 3076
  52.0 122.9 %copy-start.2 = (bf16[32,128]{1,0:T(8,128)(2,1)S(1)}, bf16[32,128]{1,0:T(8,128)(2,1)}, u32[]{:S(2)}) copy-start(bf16[32,128]{1,0:T(8,128)(2,1)} %param.11) | copy-start | bytes 24580
  148.8 48.8 %copy-start.4 = (f32[8]{0:T(128)}, f32[8]{0:T(128)S(1)}, u32[]{:S(2)}) copy-start(f32[8]{0:T(128)S(1)} %broadcast_multiply_fusion) | copy-start | bytes 100
  174.2 23.4 %copy-start.1 = (f32[256]{0:T(256)}, f32[256]{0:T(256)S(1)}, u32[]{:S(2)}) copy-start(f32[256]{0:T(256)S(1)} %multiply_divide_fusion) | copy-start | bytes 3076
